TPU v7x, 256 devices: a whole 4x4x8 slice. The times are simulated.
256 devices in a mesh: dp: 64 (over z, x_hi, y), mp: 4 (over x_lo, core).
Axes of the slice: x: 4 (x_hi: 2, x_lo: 2; x = x_hi * 2 + x_lo), y: 4, z: 8, core: 2. Of those that a mesh axis runs over, the one named last changes fastest.
Arguments:
- gradients: bfloat16 [64, 1024, 6144], P('dp', None, 'mp'), may hold values from -128 to 128
- weights: bfloat16 [1024, 6144], P(None, 'mp'), may hold values from -3 to 3
- master: float32 [1024, 6144], P('dp', 'mp'), may hold values from -6 to 6
- moment_one: float32 [1024, 6144], P('dp', 'mp'), may hold values from -6 to 6
- moment_two: float32 [1024, 6144], P('dp', 'mp'), may hold values from 0.25 to 4
- group_ids: int32 [1024], replicated, may hold values from 0 to 31, never falling along the last dimension, each value on 1 to 64 neighbouring positions
Outputs:
- new_weights: bfloat16 [1024, 6144], P(None, 'mp')
- new_master: float32 [1024, 6144], P('dp', 'mp')
- new_first: float32 [1024, 6144], P('dp', 'mp')
- new_second: float32 [1024, 6144], P('dp', 'mp')
Inputs may be any that keep to these rules, and one draw needn't show every extreme that they name: `group_ids`: group numbers never fall along the rows; each group has 1 to 64 rows and every group is present.
All inputs are finite; a program needn't handle non-finite values.
Results may differ from a plain program's by a relative error of at most 0.001.
The roundings to bfloat16 on the way count: a program that leaves them out, or rounds other values in their place, can miss the bound.
Values may be sent and summed in bfloat16 or wider, within the bound.
A program may use at most 64 MiB of HBM per device.

v0:
```python
import functools
import jax
import jax.numpy as jnp
from jax import lax
from jax.sharding import Mesh
from jax.sharding import PartitionSpec as P

DP = ("dp_0", "dp_1", "dp_2")
DP_MP = ("dp_0", "dp_1", "dp_2", "mp_0", "mp_1")
MP = ("mp_0", "mp_1")
beta_one = 0.9
beta_two = 0.999
adam_eps = 1e-06
weight_decay = 0.01
learn_rate = 0.04
step_count = 100


def split_up(x, dim, count):
    before, after = (x.shape[:dim], x.shape[dim + 1 :])
    return jnp.moveaxis(x.reshape(*before, count, -1, *after), dim, 0)


def summed_on_arrival(x, axis, dim):
    parts = split_up(x, dim, lax.axis_size(axis))
    arrived = lax.all_to_all(parts, axis, split_axis=0, concat_axis=0, tiled=True)
    return arrived.astype(jnp.float32).sum(axis=0)


def by_axis(x, axes):
    return functools.reduce(lax.psum, axes, x)


def joined_along(parts, dim):
    dims = list(parts.shape[1:])
    dims[dim] *= parts.shape[0]
    return jnp.moveaxis(parts, 0, dim).reshape(dims)


def gather_in_order(x, axes, sequence):
    parts = x[None]
    for k in sequence:
        parts = lax.all_gather(parts, axes[k], axis=0, tiled=True)
    current = [lax.axis_size(axes[k]) for k in reversed(sequence)]
    parts = parts.reshape(*current, *x.shape)
    turned = sorted(range(len(sequence)), key=lambda place: sequence[len(sequence) - 1 - place])
    return parts.transpose(*turned, *range(len(sequence), parts.ndim)).reshape(-1, *x.shape)


def whole_of(x, axes, sequence, dim):
    return joined_along(gather_in_order(x, axes, sequence), dim)


def on_device(gradients, weights, master, moment_one, moment_two, group_ids):
    owned_rows = master.shape[0]
    rows_all = weights.shape[0]
    groups = rows_all // 32
    replicas = lax.axis_size(DP)
    my_index = lax.axis_index(DP)
    first_own = my_index * owned_rows
    my_groups = lax.dynamic_slice_in_dim(group_ids, first_own, owned_rows, 0)
    member = (my_groups[:, None] == jnp.arange(groups, dtype=jnp.int32)[None, :]).astype(
        jnp.float32
    )
    weight_rows = jnp.dot(jnp.sum(master * master, axis=1), member, precision=lax.Precision.HIGHEST)
    local_grad = gradients[0]
    summed = summed_on_arrival(local_grad.astype(jnp.float32).astype(jnp.bfloat16), DP, 0)
    grad_mean = summed / replicas
    new_first = beta_one * moment_one + (1.0 - beta_one) * grad_mean
    new_second = beta_two * moment_two + (1.0 - beta_two) * grad_mean * grad_mean
    correct_one = 1.0 - beta_one**step_count
    correct_two = 1.0 - beta_two**step_count
    update = (
        new_first / correct_one / (jnp.sqrt(new_second / correct_two) + adam_eps)
        + weight_decay * master
    )
    update_rows = jnp.dot(jnp.sum(update * update, axis=1), member, precision=lax.Precision.HIGHEST)
    weight_sq, update_sq = (by_axis(weight_rows, DP_MP), by_axis(update_rows, DP_MP))
    trust_ratio = jnp.sqrt(weight_sq / (update_sq + 1e-06))
    row_ratio = jnp.dot(member, trust_ratio, precision=lax.Precision.HIGHEST)
    step_size = learn_rate * row_ratio[:, None] * update
    new_master = master - step_size
    delta_bf = (-step_size).astype(jnp.bfloat16)
    new_weights = (
        weights.astype(jnp.float32) + whole_of(delta_bf, DP, (1, 0, 2), 0).astype(jnp.float32)
    ).astype(jnp.bfloat16)
    return (new_weights, new_master, new_first, new_second)


def solution(mesh):
    torus = Mesh(mesh.devices.reshape(8, 2, 4, 2, 2), ("dp_0", "dp_1", "dp_2", "mp_0", "mp_1"))
    placed = (P(DP, None, MP), P(None, MP), P(DP, MP), P(DP, MP), P(DP, MP), P())
    return jax.shard_map(
        on_device,
        mesh=torus,
        in_specs=placed,
        out_specs=(P(None, MP), P(DP, MP), P(DP, MP), P(DP, MP)),
        check_vma=False,
    )
```

profile of v0, /device:TPU:1, one launch (start us, length us, event | category | flops | bytes accessed | tf_op | source)
XLA Modules:
  0.0 223.6 jit_solution(12461575750495941655)
XLA Ops:
  7.2 15.1 %all-to-all-start = ((bf16[64,16,1536]{2,1,0:T(8,128)(2,1)}), bf16[64,16,1536]{2,1,0:T(8,128)(2,1)S(1)}, u32[]{:S(2)}, u32[]{:S(2)}) async-start(bf16[64,16,1536]{2,1,0:T(8,128)(2,1)} %bitcast.27), calls=%async_computation | async-start | bytes 6291456 | tf_op jit(solution)/shard_map/all_to_all | solution.py:26
  22.3 0.0 copy-start.1
  22.3 0.0 all-gather.3.cloned.1.call-start
  22.4 0.8 dynamic_slice.3
  23.2 69.7 %all-to-all-done = bf16[64,16,1536]{2,1,0:T(8,128)(2,1)S(1)} async-done(((bf16[64,16,1536]{2,1,0:T(8,128)(2,1)}), bf16[64,16,1536]{2,1,0:T(8,128)(2,1)S(1)}, u32[]{:S(2)}, u32[]{:S(2)}) %all-to-all-start) | async-done | bytes 3145760 | tf_op jit(solution)/shard_map/all_to_all | solution.py:26
  92.9 0.5 convert_reduce_fusion
  93.4 0.9 multiply_reduce_fusion
  94.2 0.2 convolution_bitcast_fusion.1
  94.4 0.2 convolution_bitcast_fusion.2
  94.6 13.4 %all-reduce = (f32[32]{0:T(128)S(1)}, f32[32]{0:T(128)S(1)}) all-reduce(f32[32]{0:T(128)S(1)} %convolution_bitcast_fusion.2, f32[32]{0:T(128)S(1)} %convolution_bitcast_fusion.1), channel_id=1, replica_groups=mesh['dp_0'=8,'dp_1'=2,'dp_2'=4,'mp_0'=2,'mp_1'=2] {'dp_0'}, use_global_device_ids=true, to_apply=%region_1.0 | all-reduce | flops 64 | bytes 512 | tf_op jit(solution)/shard_map/psum | solution.py:31
  108.0 5.3 %all-reduce.4 = (f32[32]{0:T(128)S(1)}, f32[32]{0:T(128)S(1)}) all-reduce(f32[32]{0:T(128)S(1)} %get-tuple-element.4, f32[32]{0:T(128)S(1)} %get-tuple-element.5), channel_id=1, replica_groups=mesh['dp_0'=8,'dp_1'=2,'dp_2'=4,'mp_0'=2,'mp_1'=2] {'dp_1'}, use_global_device_ids=true, to_apply=%region_2.0 | all-reduce | flops 64 | bytes 512 | tf_op jit(solution)/shard_map/psum | solution.py:31
  113.3 7.7 %all-reduce.1 = (f32[32]{0:T(128)S(1)}, f32[32]{0:T(128)S(1)}) all-reduce(f32[32]{0:T(128)S(1)} %get-tuple-element.12, f32[32]{0:T(128)S(1)} %get-tuple-element.13), channel_id=1, replica_groups=mesh['dp_0'=8,'dp_1'=2,'dp_2'=4,'mp_0'=2,'mp_1'=2] {'dp_2'}, use_global_device_ids=true, to_apply=%region_3.0 | all-reduce | flops 64 | bytes 512 | tf_op jit(solution)/shard_map/psum | solution.py:31
  120.9 3.8 %all-reduce.3 = (f32[32]{0:T(128)S(1)}, f32[32]{0:T(128)S(1)}) all-reduce(f32[32]{0:T(128)S(1)} %get-tuple-element.6, f32[32]{0:T(128)S(1)} %get-tuple-element.7), channel_id=1, replica_groups=mesh['dp_0'=8,'dp_1'=2,'dp_2'=4,'mp_0'=2,'mp_1'=2] {'mp_0'}, use_global_device_ids=true, to_apply=%region_4.0 | all-reduce | flops 64 | bytes 512 | tf_op jit(solution)/shard_map/psum | solution.py:31
  124.7 11.8 %all-reduce.2 = (f32[32]{0:T(128)S(1)}, f32[32]{0:T(128)S(1)}) all-reduce(f32[32]{0:T(128)S(1)} %get-tuple-element.10, f32[32]{0:T(128)S(1)} %get-tuple-element.11), channel_id=1, replica_groups=mesh['dp_0'=8,'dp_1'=2,'dp_2'=4,'mp_0'=2,'mp_1'=2] {'mp_1'}, use_global_device_ids=true, to_apply=%region_5.0 | all-reduce | flops 64 | bytes 512 | tf_op jit(solution)/shard_map/psum | solution.py:31
  136.5 0.2 fusion.1
  136.7 0.7 multiply_subtract_fusion
  137.4 5.1 %all-gather = bf16[32,1536]{1,0:T(8,128)(2,1)S(1)} all-gather(bf16[16,1536]{1,0:T(8,128)(2,1)S(1)} %get-tuple-element.19), channel_id=2, replica_groups=mesh['dp_0'=8,'dp_1'=2,'dp_2'=4,'mp_0'=2,'mp_1'=2] {'dp_1'}, dimensions={0}, use_global_device_ids=true | all-gather | bytes 147456 | tf_op jit(solution)/shard_map/all_gather | solution.py:43
  142.5 22.8 %all_gather.10 = bf16[16,16,1536]{2,1,0:T(8,128)(2,1)} all-gather(bf16[2,16,1536]{2,1,0:T(8,128)(2,1)S(1)} %bitcast.29), channel_id=1, replica_groups=mesh['dp_0'=8,'dp_1'=2,'dp_2'=4,'mp_0'=2,'mp_1'=2] {'dp_0'}, dimensions={0}, use_global_device_ids=true | all-gather | bytes 884736 | tf_op jit(solution)/shard_map/all_gather | solution.py:43
  165.3 0.0 all-gather.3.cloned.1.call-update
  165.4 44.0 %all-gather.3.cloned.1.call-done = bf16[64,16,1536]{2,1,0:T(8,128)(2,1)} async-done(((bf16[16,16,1536]{2,1,0:T(8,128)(2,1)}), bf16[64,16,1536]{2,1,0:T(8,128)(2,1)}) %all-gather.3.cloned.1.call-update) | async-done | bytes 3145744 | tf_op jit(solution)/shard_map/all_gather | solution.py:43
  209.4 2.8 %convert_bitcast_fusion = f32[8,2,4,16,1536]{4,3,1,0,2:T(8,128)S(1)} fusion(bf16[4,8,2,16,1536]{4,3,2,1,0:T(8,128)(2,1)} %bitcast.28), kind=kLoop, calls=%fused_computation | loop fusion | flops 1572864 | bytes 9437184 | tf_op jit(solution)/shard_map/convert_element_type | solution.py:85
  212.2 0.4 copy.11
  212.6 1.4 copy-done
  214.1 2.7 %fusion = bf16[1024,1536]{1,0:T(8,128)(2,1)} fusion(f32[8,2,4,16,1536]{4,3,2,1,0:T(8,128)S(1)} %copy.11, bf16[1024,1536]{1,0:T(8,128)(2,1)S(1)} %copy-done), kind=kLoop, calls=%fused_computation.2 | loop fusion | flops 4718592 | bytes 12582912 | tf_op jit(solution)/shard_map/convert_element_type | solution.py:86
  (6 shorter events, 0.0 us)
Async XLA Ops:
  7.2 85.7 %all-to-all-start = ((bf16[64,16,1536]{2,1,0:T(8,128)(2,1)}), bf16[64,16,1536]{2,1,0:T(8,128)(2,1)S(1)}, u32[]{:S(2)}, u32[]{:S(2)}) async-start(bf16[64,16,1536]{2,1,0:T(8,128)(2,1)} %bitcast.27), calls=%async_computation | async-start | bytes 6291456 | tf_op jit(solution)/shard_map/all_to_all | solution.py:26
  22.3 71.1 %copy-start.1 = (f32[16,1536]{1,0:T(8,128)S(1)}, f32[16,1536]{1,0:T(8,128)}, u32[]{:S(2)}) copy-start(f32[16,1536]{1,0:T(8,128)} %param.8) | copy-start | bytes 294916
  22.3 71.1 %copy-start.2 = (f32[16,1536]{1,0:T(8,128)S(1)}, f32[16,1536]{1,0:T(8,128)}, u32[]{:S(2)}) copy-start(f32[16,1536]{1,0:T(8,128)} %param.9) | copy-start | bytes 294916
  22.3 71.1 %copy-start.3 = (f32[16,1536]{1,0:T(8,128)S(1)}, f32[16,1536]{1,0:T(8,128)}, u32[]{:S(2)}) copy-start(f32[16,1536]{1,0:T(8,128)} %param.10) | copy-start | bytes 294916
  22.3 187.1 %all-gather.3.cloned.1.call-start = ((), (), s32[]{:S(2)}) async-start(), calls=%async_computation.1 | async-start | bytes 3932160 | tf_op jit(solution)/shard_map/all_gather | solution.py:43
  212.2 1.9 copy-start
Sparse Core Ops, SparseCore 0:
  165.5 43.8 all-gather.2
where the time goes:
time: 224 us
  waiting for transfers between devices  114 us (51%)
  blocking collectives  69.8 us (31%)
  starting transfers between devices  15.2 us (7%)
  between operations  14.1 us (6%)
  other arithmetic  7.49 us (3%)
  local copies, waits for them, and re-layouts  2.71 us (1%)
    all_to_all x1, waiting for transfers between devices, summed_on_arrival(): lax.all_to_all(parts, axis, split_axis=0, concat_axis=0, tiled=True)  69.7 us
    all_gather x1, waiting for transfers between devices, gather_in_order(): parts = lax.all_gather(parts, axes[k], axis=0, tiled=True)  44 us
    psum x5, blocking collectives, by_axis(): return functools.reduce(lax.psum, axes, x)  41.9 us
    all_gather x2, blocking collectives, gather_in_order(): parts = lax.all_gather(parts, axes[k], axis=0, tiled=True)  27.9 us
    all_to_all x1, starting transfers between devices, summed_on_arrival(): lax.all_to_all(parts, axis, split_axis=0, concat_axis=0, tiled=True)  15.1 us
  transfers between devices with their start and end apart: 2, of which 2 were waited for; matrix products, arithmetic and copies ran while one was open for 0% of the time, Pallas kernels for 0%

commit v1 on v0

--- a/solution.py
+++ b/solution.py
@@ -4,6 +4,7 @@
 from jax import lax
 from jax.sharding import Mesh
 from jax.sharding import PartitionSpec as P
+from jax.lax import all_to_all, axis_size
 
 DP = ("dp_0", "dp_1", "dp_2")
 DP_MP = ("dp_0", "dp_1", "dp_2", "mp_0", "mp_1")
@@ -40,7 +41,10 @@
 def gather_in_order(x, axes, sequence):
     parts = x[None]
     for k in sequence:
-        parts = lax.all_gather(parts, axes[k], axis=0, tiled=True)
+        obj = axes[k]
+        parts = jnp.concatenate(
+            all_to_all(jnp.stack([parts] * axis_size(obj), axis=0), obj, 0, 0), axis=0
+        )
     current = [lax.axis_size(axes[k]) for k in reversed(sequence)]
     parts = parts.reshape(*current, *x.shape)
     turned = sorted(range(len(sequence)), key=lambda place: sequence[len(sequence) - 1 - place])

time: 224 us -> 209 us (0.933); the launches traced: 224 us -> 206 us
  waiting for transfers between devices: 114 us -> 69.7 us
  blocking collectives: 69.8 us -> 111 us
  between operations: 14.1 us -> 0.74 us
    all_to_all x0 -> x3, blocking collectives: none -> 69.1 us  [gather_in_order(): all_to_all(jnp.stack([parts] * axis_size(obj), axis=0), obj, 0, 0)]
    all_gather x1 -> x0, waiting for transfers between devices: 44 us -> none  [gather_in_order(): parts = lax.all_gather(parts, axes[k], axis=0, tiled=True)]
    all_gather x2 -> x0, blocking collectives: 27.9 us -> none  [gather_in_order(): parts = lax.all_gather(parts, axes[k], axis=0, tiled=True)]
  transfers between devices with their start and end apart: 2 -> 1, of which waited for: 2 -> 1; matrix products, arithmetic and copies ran while one was open for 0% -> 0% of each run, Pallas kernels for 0% -> 0%
where the time goes in v1:
time: 209 us; the launch traced here: 206 us
  blocking collectives  111 us (53%)
  waiting for transfers between devices  69.7 us (33%)
  starting transfers between devices  15.1 us (7%)
  other arithmetic  5.61 us (3%)
  local copies, waits for them, and re-layouts  3.17 us (2%)
    all_to_all x1, waiting for transfers between devices, summed_on_arrival(): lax.all_to_all(parts, axis, split_axis=0, concat_axis=0, tiled=True)  69.7 us
    all_to_all x3, blocking collectives, gather_in_order(): all_to_all(jnp.stack([parts] * axis_size(obj), axis=0), obj, 0, 0)  69.1 us
    psum x5, blocking collectives, by_axis(): return functools.reduce(lax.psum, axes, x)  41.9 us
    all_to_all x1, starting transfers between devices, summed_on_arrival(): lax.all_to_all(parts, axis, split_axis=0, concat_axis=0, tiled=True)  15.1 us
  transfers between devices with their start and end apart: 1, of which 1 were waited for; matrix products, arithmetic and copies ran while one was open for 0% of the time, Pallas kernels for 0%

profile of v1, /device:TPU:1, one launch (start us, length us, event | category | flops | bytes accessed | tf_op | source)
XLA Modules:
  0.0 205.9 jit_solution(12981610433176750513)
XLA Ops:
  0.6 15.1 %all-to-all-start = ((bf16[64,16,1536]{2,1,0:T(8,128)(2,1)}), bf16[64,16,1536]{2,1,0:T(8,128)(2,1)S(1)}, u32[]{:S(2)}, u32[]{:S(2)}) async-start(bf16[64,16,1536]{2,1,0:T(8,128)(2,1)} %bitcast.31), calls=%async_computation | async-start | bytes 6291456 | tf_op jit(solution)/shard_map/all_to_all | solution.py:27
  15.8 0.0 copy-start.1
  15.8 0.8 dynamic_slice.3
  16.6 69.7 %all-to-all-done = bf16[64,16,1536]{2,1,0:T(8,128)(2,1)S(1)} async-done(((bf16[64,16,1536]{2,1,0:T(8,128)(2,1)}), bf16[64,16,1536]{2,1,0:T(8,128)(2,1)S(1)}, u32[]{:S(2)}, u32[]{:S(2)}) %all-to-all-start) | async-done | bytes 3145760 | tf_op jit(solution)/shard_map/all_to_all | solution.py:27
  86.4 0.5 convert_reduce_fusion
  86.8 0.9 multiply_reduce_fusion
  87.7 0.2 convolution_bitcast_fusion.1
  87.9 0.2 convolution_bitcast_fusion.2
  88.1 13.4 %all-reduce = (f32[32]{0:T(128)S(1)}, f32[32]{0:T(128)S(1)}) all-reduce(f32[32]{0:T(128)S(1)} %convolution_bitcast_fusion.2, f32[32]{0:T(128)S(1)} %convolution_bitcast_fusion.1), channel_id=1, replica_groups=mesh['dp_0'=8,'dp_1'=2,'dp_2'=4,'mp_0'=2,'mp_1'=2] {'dp_0'}, use_global_device_ids=true, to_apply=%region_1.0 | all-reduce | flops 64 | bytes 512 | tf_op jit(solution)/shard_map/psum | solution.py:32
  101.5 5.3 %all-reduce.4 = (f32[32]{0:T(128)S(1)}, f32[32]{0:T(128)S(1)}) all-reduce(f32[32]{0:T(128)S(1)} %get-tuple-element.4, f32[32]{0:T(128)S(1)} %get-tuple-element.5), channel_id=1, replica_groups=mesh['dp_0'=8,'dp_1'=2,'dp_2'=4,'mp_0'=2,'mp_1'=2] {'dp_1'}, use_global_device_ids=true, to_apply=%region_2.0 | all-reduce | flops 64 | bytes 512 | tf_op jit(solution)/shard_map/psum | solution.py:32
  106.7 7.7 %all-reduce.1 = (f32[32]{0:T(128)S(1)}, f32[32]{0:T(128)S(1)}) all-reduce(f32[32]{0:T(128)S(1)} %get-tuple-element.12, f32[32]{0:T(128)S(1)} %get-tuple-element.13), channel_id=1, replica_groups=mesh['dp_0'=8,'dp_1'=2,'dp_2'=4,'mp_0'=2,'mp_1'=2] {'dp_2'}, use_global_device_ids=true, to_apply=%region_3.0 | all-reduce | flops 64 | bytes 512 | tf_op jit(solution)/shard_map/psum | solution.py:32
  114.4 3.8 %all-reduce.3 = (f32[32]{0:T(128)S(1)}, f32[32]{0:T(128)S(1)}) all-reduce(f32[32]{0:T(128)S(1)} %get-tuple-element.6, f32[32]{0:T(128)S(1)} %get-tuple-element.7), channel_id=1, replica_groups=mesh['dp_0'=8,'dp_1'=2,'dp_2'=4,'mp_0'=2,'mp_1'=2] {'mp_0'}, use_global_device_ids=true, to_apply=%region_4.0 | all-reduce | flops 64 | bytes 512 | tf_op jit(solution)/shard_map/psum | solution.py:32
  118.2 11.8 %all-reduce.2 = (f32[32]{0:T(128)S(1)}, f32[32]{0:T(128)S(1)}) all-reduce(f32[32]{0:T(128)S(1)} %get-tuple-element.10, f32[32]{0:T(128)S(1)} %get-tuple-element.11), channel_id=1, replica_groups=mesh['dp_0'=8,'dp_1'=2,'dp_2'=4,'mp_0'=2,'mp_1'=2] {'mp_1'}, use_global_device_ids=true, to_apply=%region_5.0 | all-reduce | flops 64 | bytes 512 | tf_op jit(solution)/shard_map/psum | solution.py:32
  130.0 0.2 fusion.1
  130.2 0.7 multiply_subtract_fusion
  130.9 8.4 %all_to_all.20 = bf16[2,1,16,1536]{3,2,1,0:T(8,128)(2,1)S(1)} all-to-all(bf16[2,1,16,1536]{3,2,1,0:T(8,128)(2,1)S(1)} %pad_maximum_fusion), channel_id=1, replica_groups=mesh['dp_0'=8,'dp_1'=2,'dp_2'=4,'mp_0'=2,'mp_1'=2] {'dp_1'}, dimensions={0} | all-to-all | bytes 196608 | tf_op jit(solution)/shard_map/all_to_all | solution.py:46
  139.4 0.1 stack.10
  139.4 24.2 %all_to_all.21 = bf16[8,2,16,1536]{3,2,1,0:T(8,128)(2,1)S(1)} all-to-all(bf16[8,2,16,1536]{3,2,1,0:T(8,128)(2,1)S(1)} %stack.10), channel_id=1, replica_groups=mesh['dp_0'=8,'dp_1'=2,'dp_2'=4,'mp_0'=2,'mp_1'=2] {'dp_0'}, dimensions={0} | all-to-all | bytes 1572864 | tf_op jit(solution)/shard_map/all_to_all | solution.py:46
  163.6 0.4 stack.11
  164.0 36.4 %all_to_all.22 = bf16[4,16,16,1536]{3,2,1,0:T(8,128)(2,1)S(1)} all-to-all(bf16[4,16,16,1536]{3,2,1,0:T(8,128)(2,1)S(1)} %stack.11), channel_id=1, replica_groups=mesh['dp_0'=8,'dp_1'=2,'dp_2'=4,'mp_0'=2,'mp_1'=2] {'dp_2'}, dimensions={0} | all-to-all | bytes 6291456 | tf_op jit(solution)/shard_map/all_to_all | solution.py:46
  200.4 0.9 convert_bitcast_fusion
  201.3 0.4 copy.10
  201.8 1.4 copy-done
  203.2 2.7 %fusion = bf16[1024,1536]{1,0:T(8,128)(2,1)} fusion(f32[8,2,4,16,1536]{4,3,2,1,0:T(8,128)S(1)} %copy.10, bf16[1024,1536]{1,0:T(8,128)(2,1)S(1)} %copy-done), kind=kLoop, calls=%fused_computation.2 | loop fusion | flops 4718592 | bytes 12582912 | tf_op jit(solution)/shard_map/convert_element_type | solution.py:90
  (7 shorter events, 0.0 us)
Async XLA Ops:
  0.6 85.7 %all-to-all-start = ((bf16[64,16,1536]{2,1,0:T(8,128)(2,1)}), bf16[64,16,1536]{2,1,0:T(8,128)(2,1)S(1)}, u32[]{:S(2)}, u32[]{:S(2)}) async-start(bf16[64,16,1536]{2,1,0:T(8,128)(2,1)} %bitcast.31), calls=%async_computation | async-start | bytes 6291456 | tf_op jit(solution)/shard_map/all_to_all | solution.py:27
  15.8 71.1 %copy-start.1 = (f32[16,1536]{1,0:T(8,128)S(1)}, f32[16,1536]{1,0:T(8,128)}, u32[]{:S(2)}) copy-start(f32[16,1536]{1,0:T(8,128)} %param.8) | copy-start | bytes 294916
  15.8 71.1 %copy-start.2 = (f32[16,1536]{1,0:T(8,128)S(1)}, f32[16,1536]{1,0:T(8,128)}, u32[]{:S(2)}) copy-start(f32[16,1536]{1,0:T(8,128)} %param.9) | copy-start | bytes 294916
  15.8 71.1 %copy-start.3 = (f32[16,1536]{1,0:T(8,128)S(1)}, f32[16,1536]{1,0:T(8,128)}, u32[]{:S(2)}) copy-start(f32[16,1536]{1,0:T(8,128)} %param.10) | copy-start | bytes 294916
  201.3 1.9 copy-start
